TPU v7x, 32 devices: a whole 2x2x4 slice. The times are simulated.
32 devices in a mesh: wide: 16 (over z, y, core), narrow: 2 (over x).
Axes of the slice: x: 2, y: 2, z: 4, core: 2. Of those that a mesh axis runs over, the one named last changes fastest.
Arguments:
- src_field: bfloat16 [2, 16, 65536], P(None, 'narrow', 'wide'), may hold values from -6 to 6
- src_depth: int32 [65536], P(('wide', 'narrow')), may hold values from 0 to 16, as said below
- packed_counts: int32 [4096, 64, 128], P(('wide', 'narrow')), may hold values from 0 to 100664832, as said below
- pair_source: int32 [4096], P(('wide', 'narrow')), may hold values from 0 to 15
- pair_home: int32 [4096], P(('wide', 'narrow')), may hold values from 0 to 1023, as said below
- pair_count: int32 [32], P(('wide', 'narrow')), may hold values from 64 to 128, as said below
Outputs:
- remapped: bfloat16 [2, 16, 131072], P(None, 'narrow', 'wide')
Inputs may be any that keep to these rules, and one draw needn't show every extreme that they name: `src_depth`: depth 0 marks a dry source cell. `packed_counts`: word (p, i, j) holds count (p, i, j) plus 65536 times count (p, i + 64, j); every count lies between 0 and 1536. The target block pair_home[p] is held by wide index pair_home[p] // 64, which differs by at most 2, counted cyclically over the wide axis, from the wide index of the device that holds pair p. Among the 128 pairs of one device at most 51 have target blocks on one wide index, and on some wide index exactly 51 live pairs of that device. A device's pairs from position pair_count[d] on are padding; some device has all 128 live.
All inputs are finite; a program needn't handle non-finite values.
Results may differ from a plain program's by a relative error of at most 0.0054.
Values may be sent and summed in bfloat16 or wider, within the bound.
A program may use at most 64 MiB of HBM per device.

v0:
```python
import jax
import jax.numpy as jnp
from jax import lax
from jax.sharding import PartitionSpec as P

DENOM = 256
REACH = 2
TB_DEV = 64
wet_limit = 0.001


def passed_along(block, axis, distance):
    devices = range(lax.axis_size(axis))
    route = [((i - distance) % len(devices), i) for i in devices]
    return lax.ppermute(block, axis, route)


def unpack_counts(packed_words):
    return jnp.concatenate([packed_words % 65536, packed_words // 65536], axis=-2)


def block_sums(targets, received, block_count):
    owners = jnp.arange(block_count, dtype=jnp.int32)
    select = (targets[:, None] == owners[None, :]).astype(jnp.bfloat16)
    return jnp.einsum("rq,rlcb->lcqb", select, received, preferred_element_type=jnp.float32)


def per_device(src_field, src_depth, packed_counts, pair_source, pair_home, pair_count):
    narrow_size = lax.axis_size("narrow")
    wide_size = lax.axis_size("wide")
    field_vars = src_field.shape[0]
    components = field_vars + 1
    block_cells = packed_counts.shape[2]
    own_cells = src_depth.shape[0]
    own_tiles = own_cells // block_cells
    pair_slots = pair_source.shape[0]
    offset_count = 2 * REACH + 1
    capacity = max(2, 2 * pair_slots // offset_count)
    own_field = lax.all_to_all(src_field, "narrow", split_axis=2, concat_axis=1, tiled=True)
    levels = own_field.shape[1]
    part_levels = levels // narrow_size
    level_ids = jnp.arange(levels, dtype=jnp.int32)
    wet_levels = level_ids[:, None] < src_depth[None, :]
    masked = jnp.where(wet_levels[None, :, :], own_field, jnp.zeros_like(own_field))
    stacked = jnp.concatenate(
        [jnp.transpose(masked, (1, 0, 2)), wet_levels.astype(jnp.bfloat16)[:, None, :]], axis=1
    )
    by_tile = jnp.transpose(stacked.reshape(levels * components, own_tiles, block_cells), (1, 0, 2))
    picked = jnp.take(by_tile, pair_source, axis=0)
    weight = (unpack_counts(packed_counts).astype(jnp.float32) / DENOM).astype(jnp.bfloat16)
    pair_terms = lax.dot_general(
        picked, weight, (((2,), (2,)), ((0,), (0,))), preferred_element_type=jnp.float32
    )
    pair_terms = pair_terms.astype(jnp.bfloat16)
    is_live = jnp.arange(pair_slots, dtype=jnp.int32) < pair_count[0]
    wide_index = lax.axis_index("wide")
    destination = pair_home // TB_DEV
    local_block = pair_home % TB_DEV
    offset_index = (destination - wide_index + REACH + wide_size) % wide_size
    bound_for = (
        (offset_index[:, None] == jnp.arange(offset_count, dtype=jnp.int32)[None, :])
        & is_live[:, None]
    ).astype(jnp.int32)
    before = jnp.cumsum(bound_for, axis=0) - bound_for
    position = jnp.sum(before * bound_for, axis=1)
    slot_index = jnp.where(is_live, offset_index * capacity + position, offset_count * capacity)
    outgoing = (
        jnp.zeros((offset_count * capacity, levels * components, block_cells), jnp.bfloat16)
        .at[slot_index]
        .set(pair_terms, mode="drop")
    )
    targets = (
        jnp.full((offset_count * capacity,), TB_DEV, jnp.int32)
        .at[slot_index]
        .set(local_block, mode="drop")
    )
    outgoing = outgoing.reshape(offset_count, capacity, levels, components, block_cells)
    targets = targets.reshape(offset_count, capacity)
    shift_list = [shift_by for shift_by in range(-REACH, REACH + 1) if shift_by != 0]
    partial_value = block_sums(targets[REACH], outgoing[REACH], TB_DEV)
    for shift_by in shift_list:
        moved_terms, moved_owners = passed_along(
            (outgoing[REACH + shift_by], targets[REACH + shift_by]), "wide", shift_by
        )
        partial_value = partial_value + block_sums(moved_owners, moved_terms, TB_DEV)
    block_totals = lax.psum_scatter(partial_value, "narrow", scatter_dimension=0, tiled=True)
    numerators = block_totals[:, :field_vars]
    wet_total = block_totals[:, field_vars]
    covered = wet_total > wet_limit
    safe_wet = jnp.where(covered, wet_total, jnp.ones_like(wet_total))
    result = jnp.where(covered[:, None], numerators / safe_wet[:, None], jnp.zeros_like(numerators))
    result = jnp.transpose(result, (1, 0, 2, 3)).reshape(
        field_vars, part_levels, TB_DEV * block_cells
    )
    return result.astype(jnp.bfloat16)


def solution(mesh):
    placed = (
        P(None, "narrow", "wide"),
        P(("wide", "narrow")),
        P(("wide", "narrow"), None, None),
        P(("wide", "narrow")),
        P(("wide", "narrow")),
        P(("wide", "narrow")),
    )
    return jax.shard_map(
        per_device, mesh=mesh, in_specs=placed, out_specs=P(None, "narrow", "wide"), check_vma=False
    )
```

profile of v0, /device:TPU:0, one launch (start us, length us, event | category | flops | bytes accessed | tf_op | source)
XLA Modules:
  0.0 141.5 jit_solution(15521793403621437424)
XLA Ops:
  6.5 4.4 %copy.29 = bf16[2,8,4096]{1,0,2:T(2,128)(2,1)S(1)} copy(bf16[2,8,4096]{2,1,0:T(8,128)(2,1)} %param.6) | data formatting | bytes 262144 | tf_op args[0]
  10.9 2.8 %reshape.126 = bf16[2,2,16384]{2,1,0:T(2,128)(2,1)} reshape(bf16[4096,2,8]{2,1,0:T(2,128)(2,1)S(1)} %bitcast.60) | data formatting | bytes 262144
  13.8 4.2 %all-to-all-start = ((bf16[2,2,16384]{2,1,0:T(2,128)(2,1)}), bf16[2,2,16384]{2,1,0:T(2,128)(2,1)S(1)}, u32[]{:S(2)}, u32[]{:S(2)}) async-start(bf16[2,2,16384]{2,1,0:T(2,128)(2,1)} %reshape.126), calls=%async_computation | async-start | bytes 262144 | tf_op jit(solution)/shard_map/all_to_all | solution.py:39
  18.0 0.1 compare_convert_fusion
  18.9 0.1 fusion.29
  19.0 0.2 reduce_window_sum.11
  19.2 0.2 select_reduce_fusion
  19.4 7.1 %add_select_fusion.1 = (s32[128,64,128]{2,1,0:T(8,128)}, s32[128,64,128]{2,1,0:T(8,128)}) fusion(s32[128,64,128]{2,1,0:T(8,128)} %param.8), kind=kLoop, calls=%fused_computation.8 | loop fusion | flops 19922944 | bytes 12582912 | tf_op jit(solution)/shard_map/jit(remainder)/select_n | solution.py:19
  26.5 2.5 %reshape.127 = bf16[4096,2,8]{2,1,0:T(2,128)(2,1)S(1)} reshape(bf16[2,2,16384]{2,1,0:T(2,128)(2,1)S(1)} %all-to-all-done) | data formatting | bytes 262144
  28.9 1.4 copy.30
  30.3 0.2 fusion.27
  30.6 0.3 pad_maximum_fusion
  30.9 0.2 reshape.91
  31.1 0.9 gather_fusion
  32.0 7.7 %fusion.7 = bf16[128,48,128]{2,1,0:T(8,128)(2,1)} fusion(s32[128,64,128]{2,1,0:T(8,128)} %get-tuple-element.6, s32[128,64,128]{2,1,0:T(8,128)} %get-tuple-element.5, bf16[128,48,128]{2,1,0:T(8,128)(2,1)S(1)} %gather_fusion, pred[128]{0:T(512)(128)(4,1)S(1)} %compare_and_fusion), kind=kOutput, calls=%fused_computation.16 | convolution fusion | flops 211288064 | bytes 11534464 | tf_op jit(solution)/shard_map/dot_general | solution.py:51
  39.8 0.4 broadcast_in_dim.71
  40.2 11.8 %scatter_fusion = bf16[255,48,128]{2,1,0:T(8,128)(2,1)S(1)} fusion(bf16[255,48,128]{2,1,0:T(8,128)(2,1)S(1)} %broadcast_in_dim.71, s32[128]{0:T(128)S(1)} %compare_select_fusion.2, bf16[128,48,128]{2,1,0:T(8,128)(2,1)} %fusion.7), kind=kCustom, calls=%fused_computation.1 | custom fusion | bytes 4719104 | tf_op jit(solution)/shard_map/scatter | solution.py:70
  52.0 1.7 %fusion.52 = (bf16[51,48,128]{2,1,0:T(8,128)(2,1)}, bf16[51,48,128]{2,1,0:T(8,128)(2,1)}, bf16[51,48,128]{2,1,0:T(8,128)(2,1)S(1)}, bf16[51,48,128]{2,1,0:T(8,128)(2,1)}, bf16[51,48,128]{2,1,0:T(8,128)(2,1)}) fusion(bf16[255,48,128]{2,1,0:T(8,128)(2,1)S(1)} %scatter_fusion), kind=kLoop, calls=%fused_computation.81 | loop fusion | bytes 6266880 | tf_op jit(solution)/shard_map/slice | solution.py:83
  53.7 0.2 copy.36
  53.9 0.1 copy.37
  54.0 4.6 %collective-permute-start.2 = (bf16[51,16,3,128]{3,1,2,0:T(8,128)(2,1)S(1)}, bf16[51,16,3,128]{3,1,2,0:T(8,128)(2,1)S(1)}, u32[]{:S(2)}, u32[]{:S(2)}) collective-permute-start(bf16[51,16,3,128]{3,1,2,0:T(8,128)(2,1)S(1)} %copy.37), channel_id=1, source_target_pairs={{2,0},{4,2},{6,4},{8,6},{10,8},{12,10},{14,12},{16,14},{18,16},{20... | collective-permute-start | bytes 1880072 | tf_op jit(solution)/shard_map/ppermute | solution.py:15
  58.6 1.0 scatter_custom_fusion.1
  59.6 1.2 copy.33
  60.9 0.1 copy.34
  61.0 0.7 collective-permute-start
  61.7 0.1 fusion.53
  61.7 0.3 collective-permute-start.3
  62.0 1.4 collective-permute-start.1
  63.4 0.2 copy.39
  63.6 0.1 copy.40
  63.7 0.2 collective-permute-start.4
  64.0 0.2 copy.32
  64.1 0.5 fusion.31
  64.6 0.2 copy.42
  64.8 0.1 copy.43
  64.9 15.0 %collective-permute-done.3 = s32[51]{0:T(128)S(1)} collective-permute-done((s32[51]{0:T(128)S(1)}, s32[51]{0:T(128)S(1)}, u32[]{:S(2)}, u32[]{:S(2)}) %collective-permute-start.3) | collective-permute-done | bytes 236 | tf_op jit(solution)/shard_map/ppermute | solution.py:15
  79.9 4.8 %collective-permute-start.5 = (s32[51]{0:T(128)S(1)}, s32[51]{0:T(128)S(1)}, u32[]{:S(2)}, u32[]{:S(2)}) collective-permute-start(s32[51]{0:T(128)S(1)} %get-tuple-element.13), channel_id=1, source_target_pairs={{30,0},{0,2},{2,4},{4,6},{6,8},{8,10},{10,12},{12,14},{14,16},{16,... | collective-permute-start | bytes 620 | tf_op jit(solution)/shard_map/ppermute | solution.py:15
  84.7 0.5 fusion.19
  85.2 3.1 %collective-permute-start.7 = (s32[51]{0:T(128)S(1)}, s32[51]{0:T(128)S(1)}, u32[]{:S(2)}, u32[]{:S(2)}) collective-permute-start(s32[51]{0:T(128)S(1)} %get-tuple-element.12), channel_id=1, source_target_pairs={{28,0},{30,2},{0,4},{2,6},{4,8},{6,10},{8,12},{10,14},{12,16},{14,... | collective-permute-start | bytes 620 | tf_op jit(solution)/shard_map/ppermute | solution.py:15
  88.3 0.5 fusion.21
  88.8 0.5 fusion.17
  89.3 14.2 %collective-permute-done.7 = s32[51]{0:T(128)S(1)} collective-permute-done((s32[51]{0:T(128)S(1)}, s32[51]{0:T(128)S(1)}, u32[]{:S(2)}, u32[]{:S(2)}) %collective-permute-start.7) | collective-permute-done | bytes 236 | tf_op jit(solution)/shard_map/ppermute | solution.py:15
  103.5 1.9 %add_bitcast_fusion = f32[16,3,64,128]{3,2,1,0:T(8,128)} fusion(f32[16,3,128,64]{2,3,1,0:T(8,128)S(1)} %fusion.17, f32[16,3,128,64]{2,3,1,0:T(8,128)S(1)} %fusion.19, f32[16,3,128,64]{2,3,1,0:T(8,128)S(1)} %fusion.31, f32[16,3,128,64]{2,3,1,0:T(8,128)S(1)} %fusion.21, bf16[51,16,3,128]{3,1,2,0:T(8,128)(2,1)S(1)} %collective-permute-done.6, ...), kind=kOutput, calls=%fused_computation.17 | convolution fusion | flops 41684160 | bytes 8491212 | tf_op jit(solution)/shard_map/rq,rlcb->lcqb/dot_general | solution.py:25
  105.4 25.3 %reduce-scatter.2.cloned.1.call-done = f32[8,3,64,128]{3,2,1,0:T(8,128)} async-done(((f32[16,3,64,128]{3,2,1,0:T(8,128)}), f32[8,3,64,128]{3,2,1,0:T(8,128)}) %reduce-scatter.2.cloned.1.call-update) | async-done | bytes 786448 | tf_op jit(solution)/shard_map/reduce_scatter | solution.py:86
  130.6 1.0 fusion.25
  131.6 1.0 compare_bitcast_fusion
  132.6 1.1 fusion.26
  133.8 0.9 copy.45
  (31 shorter events, 0.3 us)
Async XLA Ops:
  6.5 11.5 %copy-start.3 = (s32[2048]{0:T(1024)S(1)}, s32[2048]{0:T(1024)}, u32[]{:S(2)}) copy-start(s32[2048]{0:T(1024)} %param.7) | copy-start | bytes 24580
  6.5 11.6 %copy-start.5 = (s32[128]{0:T(128)S(1)}, s32[128]{0:T(128)}, u32[]{:S(2)}) copy-start(s32[128]{0:T(128)} %param.9) | copy-start | bytes 1540
  6.5 12.3 %copy-start.4 = (s32[128]{0:T(128)S(1)}, s32[128]{0:T(128)}, u32[]{:S(2)}) copy-start(s32[128]{0:T(128)} %param.10) | copy-start | bytes 1540
  13.8 12.7 %all-to-all-start = ((bf16[2,2,16384]{2,1,0:T(2,128)(2,1)}), bf16[2,2,16384]{2,1,0:T(2,128)(2,1)S(1)}, u32[]{:S(2)}, u32[]{:S(2)}) async-start(bf16[2,2,16384]{2,1,0:T(2,128)(2,1)} %reshape.126), calls=%async_computation | async-start | bytes 262144 | tf_op jit(solution)/shard_map/all_to_all | solution.py:39
  18.0 112.6 %reduce-scatter.2.cloned.1.call-start = ((), (), s32[]{:S(2)}) async-start(), calls=%async_computation.2 | async-start | bytes 2359296 | tf_op jit(solution)/shard_map/reduce_scatter | solution.py:86
  53.7 9.7 %copy-start.2 = (bf16[51,48,128]{2,1,0:T(8,128)(2,1)S(1)}, bf16[51,48,128]{2,1,0:T(8,128)(2,1)}, u32[]{:S(2)}) copy-start(bf16[51,48,128]{2,1,0:T(8,128)(2,1)} %get-tuple-element.8) | copy-start | bytes 1880068
  53.9 10.1 %copy-start.1 = (bf16[51,48,128]{2,1,0:T(8,128)(2,1)S(1)}, bf16[51,48,128]{2,1,0:T(8,128)(2,1)}, u32[]{:S(2)}) copy-start(bf16[51,48,128]{2,1,0:T(8,128)(2,1)} %get-tuple-element.11) | copy-start | bytes 1880068
  54.0 30.7 %collective-permute-start.2 = (bf16[51,16,3,128]{3,1,2,0:T(8,128)(2,1)S(1)}, bf16[51,16,3,128]{3,1,2,0:T(8,128)(2,1)S(1)}, u32[]{:S(2)}, u32[]{:S(2)}) collective-permute-start(bf16[51,16,3,128]{3,1,2,0:T(8,128)(2,1)S(1)} %copy.37), channel_id=1, source_target_pairs={{2,0},{4,2},{6,4},{8,6},{10,8},{12,10},{14,12},{16,14},{18,16},{20... | collective-permute-start | bytes 1880072 | tf_op jit(solution)/shard_map/ppermute | solution.py:15
  61.0 3.7 %copy-start = (bf16[51,48,128]{2,1,0:T(8,128)(2,1)S(1)}, bf16[51,48,128]{2,1,0:T(8,128)(2,1)}, u32[]{:S(2)}) copy-start(bf16[51,48,128]{2,1,0:T(8,128)(2,1)} %get-tuple-element.7) | copy-start | bytes 1880068
  61.0 27.4 %collective-permute-start = (bf16[51,16,3,128]{3,1,2,0:T(8,128)(2,1)S(1)}, bf16[51,16,3,128]{3,1,2,0:T(8,128)(2,1)S(1)}, u32[]{:S(2)}, u32[]{:S(2)}) collective-permute-start(bf16[51,16,3,128]{3,1,2,0:T(8,128)(2,1)S(1)} %copy.34), channel_id=1, source_target_pairs={{4,0},{6,2},{8,4},{10,6},{12,8},{14,10},{16,12},{18,14},{20,16},{2... | collective-permute-start | bytes 1880072 | tf_op jit(solution)/shard_map/ppermute | solution.py:15
  61.7 18.2 %collective-permute-start.3 = (s32[51]{0:T(128)S(1)}, s32[51]{0:T(128)S(1)}, u32[]{:S(2)}, u32[]{:S(2)}) collective-permute-start(s32[51]{0:T(128)S(1)} %get-tuple-element.14), channel_id=1, source_target_pairs={{2,0},{4,2},{6,4},{8,6},{10,8},{12,10},{14,12},{16,14},{18,16},{20... | collective-permute-start | bytes 620 | tf_op jit(solution)/shard_map/ppermute | solution.py:15
  62.0 23.1 %collective-permute-start.1 = (s32[51]{0:T(128)S(1)}, s32[51]{0:T(128)S(1)}, u32[]{:S(2)}, u32[]{:S(2)}) collective-permute-start(s32[51]{0:T(128)S(1)} %get-tuple-element.15), channel_id=1, source_target_pairs={{4,0},{6,2},{8,4},{10,6},{12,8},{14,10},{16,12},{18,14},{20,16},{2... | collective-permute-start | bytes 620 | tf_op jit(solution)/shard_map/ppermute | solution.py:15
  63.7 25.1 %collective-permute-start.4 = (bf16[51,16,3,128]{3,1,2,0:T(8,128)(2,1)S(1)}, bf16[51,16,3,128]{3,1,2,0:T(8,128)(2,1)S(1)}, u32[]{:S(2)}, u32[]{:S(2)}) collective-permute-start(bf16[51,16,3,128]{3,1,2,0:T(8,128)(2,1)S(1)} %copy.40), channel_id=1, source_target_pairs={{30,0},{0,2},{2,4},{4,6},{6,8},{8,10},{10,12},{12,14},{14,16},{16,... | collective-permute-start | bytes 1880072 | tf_op jit(solution)/shard_map/ppermute | solution.py:15
  79.9 8.9 %collective-permute-start.5 = (s32[51]{0:T(128)S(1)}, s32[51]{0:T(128)S(1)}, u32[]{:S(2)}, u32[]{:S(2)}) collective-permute-start(s32[51]{0:T(128)S(1)} %get-tuple-element.13), channel_id=1, source_target_pairs={{30,0},{0,2},{2,4},{4,6},{6,8},{8,10},{10,12},{12,14},{14,16},{16,... | collective-permute-start | bytes 620 | tf_op jit(solution)/shard_map/ppermute | solution.py:15
  84.7 18.8 %collective-permute-start.6 = (bf16[51,16,3,128]{3,1,2,0:T(8,128)(2,1)S(1)}, bf16[51,16,3,128]{3,1,2,0:T(8,128)(2,1)S(1)}, u32[]{:S(2)}, u32[]{:S(2)}) collective-permute-start(bf16[51,16,3,128]{3,1,2,0:T(8,128)(2,1)S(1)} %copy.43), channel_id=1, source_target_pairs={{28,0},{30,2},{0,4},{2,6},{4,8},{6,10},{8,12},{10,14},{12,16},{14,... | collective-permute-start | bytes 1880072 | tf_op jit(solution)/shard_map/ppermute | solution.py:15
  85.2 18.3 %collective-permute-start.7 = (s32[51]{0:T(128)S(1)}, s32[51]{0:T(128)S(1)}, u32[]{:S(2)}, u32[]{:S(2)}) collective-permute-start(s32[51]{0:T(128)S(1)} %get-tuple-element.12), channel_id=1, source_target_pairs={{28,0},{30,2},{0,4},{2,6},{4,8},{6,10},{8,12},{10,14},{12,16},{14,... | collective-permute-start | bytes 620 | tf_op jit(solution)/shard_map/ppermute | solution.py:15
Sparse Core Ops, SparseCore 0:
  105.5 25.0 reduce-scatter.1
where the time goes:
time: 142 us
  waiting for transfers between devices  54.5 us (38%)
  local copies, waits for them, and re-layouts  30.4 us (21%)
  starting transfers between devices  19.4 us (14%)
  between operations  14.4 us (10%)
  matrix products  11.5 us (8%)
  other arithmetic  11.4 us (8%)
    ppermute x8, waiting for transfers between devices, passed_along(): return lax.ppermute(block, axis, route)  29.2 us
    reduce_scatter x1, waiting for transfers between devices, per_device(): lax.psum_scatter(partial_value, 'narrow', scatter_dimension=0, tiled=True)  25.3 us
    ppermute x8, starting transfers between devices, passed_along(): return lax.ppermute(block, axis, route)  15.2 us
    scatter x1, local copies, waits for them, and re-layouts, per_device(): outgoing = jnp.zeros((offset_count * capacity, levels * components, block...  11.8 us
    unnamed x15, local copies, waits for them, and re-layouts  9.68 us
    dot_general x1, matrix products, per_device(): lax.dot_general(picked, weight, (((2,), (2,)), ((0,), (0,))), preferred_e...  7.73 us
    select_n x1, other arithmetic, unpack_counts(): packed_words % 65536  7.1 us
    all_to_all x1, starting transfers between devices, per_device(): lax.all_to_all(src_field, 'narrow', split_axis=2, concat_axis=1, tiled=True)  4.23 us
  transfers between devices with their start and end apart: 10, of which 3 were waited for; matrix products, arithmetic and copies ran while one was open for 9% of the time, Pallas kernels for 0%

commit v1 on v0

--- a/solution.py
+++ b/solution.py
@@ -36,7 +36,12 @@
     pair_slots = pair_source.shape[0]
     offset_count = 2 * REACH + 1
     capacity = max(2, 2 * pair_slots // offset_count)
-    own_field = lax.all_to_all(src_field, "narrow", split_axis=2, concat_axis=1, tiled=True)
+    own_field = jnp.concatenate(
+        lax.all_to_all(
+            jnp.stack(jnp.split(src_field, lax.axis_size("narrow"), axis=2)), "narrow", 0, 0
+        ),
+        axis=1,
+    )
     levels = own_field.shape[1]
     part_levels = levels // narrow_size
     level_ids = jnp.arange(levels, dtype=jnp.int32)

time: 142 us -> 136 us (0.958)
  local copies, waits for them, and re-layouts: 30.4 us -> 20.4 us
  other arithmetic: 11.4 us -> 14.8 us
    unnamed x15 -> x6, local copies, waits for them, and re-layouts: 9.68 us -> 0.01 us
  transfers between devices with their start and end apart: 10 -> 10, of which waited for: 3 -> 3; matrix products, arithmetic and copies ran while one was open for 9% -> 12% of each run, Pallas kernels for 0% -> 0%
where the time goes in v1:
time: 136 us; the launch traced here: 135 us
  waiting for transfers between devices  54.7 us (40%)
  local copies, waits for them, and re-layouts  20.4 us (15%)
  starting transfers between devices  19.2 us (14%)
  other arithmetic  14.8 us (11%)
  between operations  14.3 us (11%)
  matrix products  11.5 us (8%)
    ppermute x8, waiting for transfers between devices, passed_along(): return lax.ppermute(block, axis, route)  29.4 us
    reduce_scatter x1, waiting for transfers between devices, per_device(): lax.psum_scatter(partial_value, 'narrow', scatter_dimension=0, tiled=True)  25.3 us
    ppermute x8, starting transfers between devices, passed_along(): return lax.ppermute(block, axis, route)  15 us
    scatter x1, local copies, waits for them, and re-layouts, per_device(): outgoing = jnp.zeros((offset_count * capacity, levels * components, block...  11.8 us
    dot_general x1, matrix products, per_device(): lax.dot_general(picked, weight, (((2,), (2,)), ((0,), (0,))), preferred_e...  7.75 us
    select_n x1, other arithmetic, unpack_counts(): packed_words % 65536  7.11 us
    all_to_all x1, starting transfers between devices, per_device(): lax.all_to_all(jnp.stack(jnp.split(src_field, lax.axis_size('narrow'), ax...  4.23 us
    dot_general x5, matrix products, block_sums(): jnp.einsum('rq,rlcb->lcqb', select, received, preferred_element_type=jnp....  3.78 us
  transfers between devices with their start and end apart: 10, of which 3 were waited for; matrix products, arithmetic and copies ran while one was open for 12% of the time, Pallas kernels for 0%

profile of v1, /device:TPU:0, one launch (start us, length us, event | category | flops | bytes accessed | tf_op | source)
XLA Modules:
  0.0 134.9 jit_solution(16890409283662385175)
XLA Ops:
  6.5 0.9 slice_bitcast_fusion.1
  7.4 0.7 pad_maximum_fusion.1
  8.1 4.2 %all-to-all-start = ((bf16[2,2,8,2048]{3,2,1,0:T(8,128)(2,1)}), bf16[2,2,8,2048]{3,2,1,0:T(8,128)(2,1)S(1)}, u32[]{:S(2)}, u32[]{:S(2)}) async-start(bf16[2,2,8,2048]{3,2,1,0:T(8,128)(2,1)} %pad_maximum_fusion.1), calls=%async_computation | async-start | bytes 262144 | tf_op jit(solution)/shard_map/all_to_all | solution.py:40
  12.3 0.7 iota_compare_fusion.1
  13.0 0.7 fusion.28
  13.8 0.7 compare_select_fusion.1
  14.4 0.7 compare_and_fusion
  15.8 0.7 and_select_fusion
  16.4 0.1 fusion.30
  16.5 0.2 reduce_window_sum.11
  16.7 0.2 select_reduce_fusion
  16.9 7.1 %add_select_fusion.1 = (s32[128,64,128]{2,1,0:T(8,128)}, s32[128,64,128]{2,1,0:T(8,128)}) fusion(s32[128,64,128]{2,1,0:T(8,128)} %param.8), kind=kLoop, calls=%fused_computation.8 | loop fusion | flops 19922944 | bytes 12582912 | tf_op jit(solution)/shard_map/jit(remainder)/select_n | solution.py:19
  24.1 0.2 copy.30
  24.2 0.2 reshape.99
  24.5 0.9 gather_fusion
  25.4 7.7 %fusion.7 = bf16[128,48,128]{2,1,0:T(8,128)(2,1)} fusion(s32[128,64,128]{2,1,0:T(8,128)} %get-tuple-element.6, s32[128,64,128]{2,1,0:T(8,128)} %get-tuple-element.5, bf16[128,48,128]{2,1,0:T(8,128)(2,1)S(1)} %gather_fusion, pred[128]{0:T(512)(128)(4,1)S(1)} %compare_and_fusion), kind=kOutput, calls=%fused_computation.16 | convolution fusion | flops 211288064 | bytes 11534464 | tf_op jit(solution)/shard_map/dot_general | solution.py:56
  33.1 0.4 broadcast_in_dim.71
  33.6 11.8 %scatter_fusion = bf16[255,48,128]{2,1,0:T(8,128)(2,1)S(1)} fusion(bf16[255,48,128]{2,1,0:T(8,128)(2,1)S(1)} %broadcast_in_dim.71, s32[128]{0:T(128)S(1)} %compare_select_fusion.2, bf16[128,48,128]{2,1,0:T(8,128)(2,1)} %fusion.7), kind=kCustom, calls=%fused_computation.1 | custom fusion | bytes 4719104 | tf_op jit(solution)/shard_map/scatter | solution.py:75
  45.4 1.7 %fusion.53 = (bf16[51,48,128]{2,1,0:T(8,128)(2,1)}, bf16[51,48,128]{2,1,0:T(8,128)(2,1)}, bf16[51,48,128]{2,1,0:T(8,128)(2,1)S(1)}, bf16[51,48,128]{2,1,0:T(8,128)(2,1)}, bf16[51,48,128]{2,1,0:T(8,128)(2,1)}) fusion(bf16[255,48,128]{2,1,0:T(8,128)(2,1)S(1)} %scatter_fusion), kind=kLoop, calls=%fused_computation.85 | loop fusion | bytes 6266880 | tf_op jit(solution)/shard_map/slice | solution.py:88
  47.1 0.2 copy.36
  47.3 0.1 copy.37
  47.4 4.6 %collective-permute-start.2 = (bf16[51,16,3,128]{3,1,2,0:T(8,128)(2,1)S(1)}, bf16[51,16,3,128]{3,1,2,0:T(8,128)(2,1)S(1)}, u32[]{:S(2)}, u32[]{:S(2)}) collective-permute-start(bf16[51,16,3,128]{3,1,2,0:T(8,128)(2,1)S(1)} %copy.37), channel_id=1, source_target_pairs={{2,0},{4,2},{6,4},{8,6},{10,8},{12,10},{14,12},{16,14},{18,16},{20... | collective-permute-start | bytes 1880072 | tf_op jit(solution)/shard_map/ppermute | solution.py:15
  52.0 1.0 scatter_custom_fusion.1
  53.0 1.2 copy.33
  54.2 0.1 copy.34
  54.3 0.7 collective-permute-start
  55.0 0.1 fusion.54
  55.1 0.3 collective-permute-start.3
  55.4 1.4 %collective-permute-start.1 = (s32[51]{0:T(128)S(1)}, s32[51]{0:T(128)S(1)}, u32[]{:S(2)}, u32[]{:S(2)}) collective-permute-start(s32[51]{0:T(128)S(1)} %get-tuple-element.17), channel_id=1, source_target_pairs={{4,0},{6,2},{8,4},{10,6},{12,8},{14,10},{16,12},{18,14},{20,16},{2... | collective-permute-start | bytes 620 | tf_op jit(solution)/shard_map/ppermute | solution.py:15
  56.8 0.2 copy.39
  57.0 0.1 copy.40
  57.2 0.2 copy.32
  57.3 0.5 fusion.32
  57.8 0.2 copy.42
  58.0 0.1 copy.43
  58.1 15.2 %collective-permute-done.3 = s32[51]{0:T(128)S(1)} collective-permute-done((s32[51]{0:T(128)S(1)}, s32[51]{0:T(128)S(1)}, u32[]{:S(2)}, u32[]{:S(2)}) %collective-permute-start.3) | collective-permute-done | bytes 236 | tf_op jit(solution)/shard_map/ppermute | solution.py:15
  73.3 4.8 %collective-permute-start.5 = (s32[51]{0:T(128)S(1)}, s32[51]{0:T(128)S(1)}, u32[]{:S(2)}, u32[]{:S(2)}) collective-permute-start(s32[51]{0:T(128)S(1)} %get-tuple-element.15), channel_id=1, source_target_pairs={{30,0},{0,2},{2,4},{4,6},{6,8},{8,10},{10,12},{12,14},{14,16},{16,... | collective-permute-start | bytes 620 | tf_op jit(solution)/shard_map/ppermute | solution.py:15
  78.1 0.5 fusion.19
  78.6 3.1 %collective-permute-start.7 = (s32[51]{0:T(128)S(1)}, s32[51]{0:T(128)S(1)}, u32[]{:S(2)}, u32[]{:S(2)}) collective-permute-start(s32[51]{0:T(128)S(1)} %get-tuple-element.14), channel_id=1, source_target_pairs={{28,0},{30,2},{0,4},{2,6},{4,8},{6,10},{8,12},{10,14},{12,16},{14,... | collective-permute-start | bytes 620 | tf_op jit(solution)/shard_map/ppermute | solution.py:15
  81.7 0.5 fusion.21
  82.2 0.5 fusion.17
  82.7 14.2 %collective-permute-done.7 = s32[51]{0:T(128)S(1)} collective-permute-done((s32[51]{0:T(128)S(1)}, s32[51]{0:T(128)S(1)}, u32[]{:S(2)}, u32[]{:S(2)}) %collective-permute-start.7) | collective-permute-done | bytes 236 | tf_op jit(solution)/shard_map/ppermute | solution.py:15
  96.9 1.9 %add_bitcast_fusion = f32[16,3,64,128]{3,2,1,0:T(8,128)} fusion(f32[16,3,128,64]{2,3,1,0:T(8,128)S(1)} %fusion.17, f32[16,3,128,64]{2,3,1,0:T(8,128)S(1)} %fusion.19, f32[16,3,128,64]{2,3,1,0:T(8,128)S(1)} %fusion.32, f32[16,3,128,64]{2,3,1,0:T(8,128)S(1)} %fusion.21, bf16[51,16,3,128]{3,1,2,0:T(8,128)(2,1)S(1)} %collective-permute-done.6, ...), kind=kOutput, calls=%fused_computation.17 | convolution fusion | flops 41684160 | bytes 8491212 | tf_op jit(solution)/shard_map/rq,rlcb->lcqb/dot_general | solution.py:25
  98.7 25.3 %reduce-scatter.2.cloned.1.call-done = f32[8,3,64,128]{3,2,1,0:T(8,128)} async-done(((f32[16,3,64,128]{3,2,1,0:T(8,128)}), f32[8,3,64,128]{3,2,1,0:T(8,128)}) %reduce-scatter.2.cloned.1.call-update) | async-done | bytes 786448 | tf_op jit(solution)/shard_map/reduce_scatter | solution.py:91
  124.0 1.0 fusion.25
  125.0 1.0 compare_bitcast_fusion
  126.0 1.1 fusion.26
  127.2 0.9 copy.45
  (24 shorter events, 0.3 us)
Async XLA Ops:
  8.1 15.9 %all-to-all-start = ((bf16[2,2,8,2048]{3,2,1,0:T(8,128)(2,1)}), bf16[2,2,8,2048]{3,2,1,0:T(8,128)(2,1)S(1)}, u32[]{:S(2)}, u32[]{:S(2)}) async-start(bf16[2,2,8,2048]{3,2,1,0:T(8,128)(2,1)} %pad_maximum_fusion.1), calls=%async_computation | async-start | bytes 262144 | tf_op jit(solution)/shard_map/all_to_all | solution.py:40
  12.3 111.7 %reduce-scatter.2.cloned.1.call-start = ((), (), s32[]{:S(2)}) async-start(), calls=%async_computation.2 | async-start | bytes 2359296 | tf_op jit(solution)/shard_map/reduce_scatter | solution.py:91
  47.1 9.7 %copy-start.2 = (bf16[51,48,128]{2,1,0:T(8,128)(2,1)S(1)}, bf16[51,48,128]{2,1,0:T(8,128)(2,1)}, u32[]{:S(2)}) copy-start(bf16[51,48,128]{2,1,0:T(8,128)(2,1)} %get-tuple-element.8) | copy-start | bytes 1880068
  47.3 9.9 %copy-start.1 = (bf16[51,48,128]{2,1,0:T(8,128)(2,1)S(1)}, bf16[51,48,128]{2,1,0:T(8,128)(2,1)}, u32[]{:S(2)}) copy-start(bf16[51,48,128]{2,1,0:T(8,128)(2,1)} %get-tuple-element.11) | copy-start | bytes 1880068
  47.4 30.7 %collective-permute-start.2 = (bf16[51,16,3,128]{3,1,2,0:T(8,128)(2,1)S(1)}, bf16[51,16,3,128]{3,1,2,0:T(8,128)(2,1)S(1)}, u32[]{:S(2)}, u32[]{:S(2)}) collective-permute-start(bf16[51,16,3,128]{3,1,2,0:T(8,128)(2,1)S(1)} %copy.37), channel_id=1, source_target_pairs={{2,0},{4,2},{6,4},{8,6},{10,8},{12,10},{14,12},{16,14},{18,16},{20... | collective-permute-start | bytes 1880072 | tf_op jit(solution)/shard_map/ppermute | solution.py:15
  54.3 3.5 %copy-start = (bf16[51,48,128]{2,1,0:T(8,128)(2,1)S(1)}, bf16[51,48,128]{2,1,0:T(8,128)(2,1)}, u32[]{:S(2)}) copy-start(bf16[51,48,128]{2,1,0:T(8,128)(2,1)} %get-tuple-element.7) | copy-start | bytes 1880068
  54.3 27.4 %collective-permute-start = (bf16[51,16,3,128]{3,1,2,0:T(8,128)(2,1)S(1)}, bf16[51,16,3,128]{3,1,2,0:T(8,128)(2,1)S(1)}, u32[]{:S(2)}, u32[]{:S(2)}) collective-permute-start(bf16[51,16,3,128]{3,1,2,0:T(8,128)(2,1)S(1)} %copy.34), channel_id=1, source_target_pairs={{4,0},{6,2},{8,4},{10,6},{12,8},{14,10},{16,12},{18,14},{20,16},{2... | collective-permute-start | bytes 1880072 | tf_op jit(solution)/shard_map/ppermute | solution.py:15
  55.1 18.2 %collective-permute-start.3 = (s32[51]{0:T(128)S(1)}, s32[51]{0:T(128)S(1)}, u32[]{:S(2)}, u32[]{:S(2)}) collective-permute-start(s32[51]{0:T(128)S(1)} %get-tuple-element.16), channel_id=1, source_target_pairs={{2,0},{4,2},{6,4},{8,6},{10,8},{12,10},{14,12},{16,14},{18,16},{20... | collective-permute-start | bytes 620 | tf_op jit(solution)/shard_map/ppermute | solution.py:15
  55.4 23.1 %collective-permute-start.1 = (s32[51]{0:T(128)S(1)}, s32[51]{0:T(128)S(1)}, u32[]{:S(2)}, u32[]{:S(2)}) collective-permute-start(s32[51]{0:T(128)S(1)} %get-tuple-element.17), channel_id=1, source_target_pairs={{4,0},{6,2},{8,4},{10,6},{12,8},{14,10},{16,12},{18,14},{20,16},{2... | collective-permute-start | bytes 620 | tf_op jit(solution)/shard_map/ppermute | solution.py:15
  57.1 25.1 %collective-permute-start.4 = (bf16[51,16,3,128]{3,1,2,0:T(8,128)(2,1)S(1)}, bf16[51,16,3,128]{3,1,2,0:T(8,128)(2,1)S(1)}, u32[]{:S(2)}, u32[]{:S(2)}) collective-permute-start(bf16[51,16,3,128]{3,1,2,0:T(8,128)(2,1)S(1)} %copy.40), channel_id=1, source_target_pairs={{30,0},{0,2},{2,4},{4,6},{6,8},{8,10},{10,12},{12,14},{14,16},{16,... | collective-permute-start | bytes 1880072 | tf_op jit(solution)/shard_map/ppermute | solution.py:15
  73.3 8.9 %collective-permute-start.5 = (s32[51]{0:T(128)S(1)}, s32[51]{0:T(128)S(1)}, u32[]{:S(2)}, u32[]{:S(2)}) collective-permute-start(s32[51]{0:T(128)S(1)} %get-tuple-element.15), channel_id=1, source_target_pairs={{30,0},{0,2},{2,4},{4,6},{6,8},{8,10},{10,12},{12,14},{14,16},{16,... | collective-permute-start | bytes 620 | tf_op jit(solution)/shard_map/ppermute | solution.py:15
  78.1 18.8 %collective-permute-start.6 = (bf16[51,16,3,128]{3,1,2,0:T(8,128)(2,1)S(1)}, bf16[51,16,3,128]{3,1,2,0:T(8,128)(2,1)S(1)}, u32[]{:S(2)}, u32[]{:S(2)}) collective-permute-start(bf16[51,16,3,128]{3,1,2,0:T(8,128)(2,1)S(1)} %copy.43), channel_id=1, source_target_pairs={{28,0},{30,2},{0,4},{2,6},{4,8},{6,10},{8,12},{10,14},{12,16},{14,... | collective-permute-start | bytes 1880072 | tf_op jit(solution)/shard_map/ppermute | solution.py:15
  78.6 18.3 %collective-permute-start.7 = (s32[51]{0:T(128)S(1)}, s32[51]{0:T(128)S(1)}, u32[]{:S(2)}, u32[]{:S(2)}) collective-permute-start(s32[51]{0:T(128)S(1)} %get-tuple-element.14), channel_id=1, source_target_pairs={{28,0},{30,2},{0,4},{2,6},{4,8},{6,10},{8,12},{10,14},{12,16},{14,... | collective-permute-start | bytes 620 | tf_op jit(solution)/shard_map/ppermute | solution.py:15
Sparse Core Ops, SparseCore 0:
  98.9 25.1 reduce-scatter.1
